TPU v7x, 32 devices: a whole 2x2x4 slice. The times are simulated.
32 devices in a mesh: seq: 8 (over z, core), tp: 4 (over y, x).
Axes of the slice: x: 2, y: 2, z: 4, core: 2. Of those that a mesh axis runs over, the one named last changes fastest.
Arguments:
- tokens: bfloat16 [1024, 8192], P('seq'), may hold values from -6 to 6
- conv_weight: float32 [4, 8192], replicated, may hold values from -3 to 3
- norm_gain: float32 [8192], replicated, may hold values from 0.25 to 1.75
- gate_weight: bfloat16 [8192, 14336], P('seq', 'tp'), may hold values from -0.0625 to 0.0625
- up_weight: bfloat16 [8192, 14336], P('seq', 'tp'), may hold values from -0.0625 to 0.0625
- down_weight: bfloat16 [14336, 8192], P('tp', 'seq'), may hold values from -0.046875 to 0.046875
Outputs:
- mixed_out: bfloat16 [1024, 8192], P(('seq', 'tp'))
All inputs are finite; a program needn't handle non-finite values.
Results may differ from a plain program's by a relative error of at most 0.03.
Values may be sent and summed in bfloat16 or wider, within the bound.
A program may use at most 128 MiB of HBM per device.

v0:
```python
import jax
import jax.numpy as jnp
from jax import lax
from jax.sharding import PartitionSpec as P


def from_behind(shard, axis, by):
    peers = lax.axis_size(axis)
    pairs = [(i, i + by) for i in range(peers) if 0 <= i + by < peers]
    return lax.ppermute(shard, axis, pairs)


def swiglu(both_sums, half_cols):
    return (jax.nn.silu(both_sums[:, :half_cols]) * both_sums[:, half_cols:]).astype(jnp.bfloat16)


def shards(tokens, conv_weight, norm_gain, gate_weight, up_weight, down_weight):
    tok_rows = tokens.shape[0]
    taps_count = conv_weight.shape[0]
    seq_count = lax.axis_size("seq")
    edge_rows = from_behind(tokens[tok_rows - (taps_count - 1) :], "seq", 1)
    extended = jnp.concatenate([edge_rows, tokens], 0).astype(jnp.float32)
    conv_out = jnp.zeros(tokens.shape, jnp.float32)
    for tap_index in range(taps_count):
        begin = taps_count - 1 - tap_index
        conv_out = conv_out + conv_weight[tap_index][None, :] * extended[begin : begin + tok_rows]
    scale_rms = lax.rsqrt(jnp.mean(conv_out * conv_out, axis=-1, keepdims=True) + 1e-05)
    normed = (conv_out * scale_rms * norm_gain[None, :]).astype(jnp.bfloat16)
    all_rows = lax.all_to_all(normed, "seq", split_axis=1, concat_axis=0, tiled=True)
    half_cols = gate_weight.shape[1]
    w_both = jnp.concatenate([gate_weight, up_weight], 1)
    gate_share = lax.psum_scatter(
        jnp.dot(all_rows, w_both, preferred_element_type=jnp.float32).astype(jnp.bfloat16),
        "seq",
        scatter_dimension=0,
        tiled=True,
    ).astype(jnp.float32)
    hidden = swiglu(gate_share, half_cols)
    out_terms = jnp.dot(
        lax.all_gather(hidden, "seq", axis=0, tiled=True),
        down_weight,
        preferred_element_type=jnp.float32,
    )
    col_width = out_terms.shape[1]
    out_terms = out_terms.reshape(seq_count, tok_rows, col_width)
    summed = lax.psum_scatter(out_terms.astype(jnp.bfloat16), "tp", scatter_dimension=1, tiled=True)
    mixed_out = lax.all_to_all(summed, "seq", split_axis=0, concat_axis=2, tiled=True)
    return mixed_out.reshape(mixed_out.shape[1], mixed_out.shape[2])


def solution(mesh):
    in_specs = (P("seq", None), P(), P(), P("seq", "tp"), P("seq", "tp"), P("tp", "seq"))
    out_specs = P(("seq", "tp"), None)
    return jax.shard_map(shards, mesh=mesh, in_specs=in_specs, out_specs=out_specs, check_vma=False)
```

profile of v0, /device:TPU:0, one launch (start us, length us, event | category | flops | bytes accessed | tf_op | source)
XLA Modules:
  0.0 409.3 jit_solution(17760382771565718284)
XLA Ops:
  6.5 0.0 reduce-scatter.3.cloned.1.call-start
  6.5 0.9 slice.34
  7.5 2.4 collective-permute-start
  9.9 1.3 fusion.13
  11.2 3.2 copy.14
  14.4 0.0 collective-permute-done
  14.4 1.9 copy.13
  16.3 3.1 maximum_convert_fusion
  19.4 0.0 copy-start
  19.4 8.7 %multiply_reduce_fusion = (f32[128]{0:T(128)S(1)}, f32[128,8192]{0,1:T(8,128)S(1)}) fusion(f32[131,8192]{0,1:T(8,128)S(1)} %maximum_convert_fusion, f32[8192]{0:T(1024)S(1)} %bitcast.26, f32[8192]{0:T(1024)S(1)} %bitcast.27, f32[8192]{0:T(1024)S(1)} %bitcast.25, f32[8192]{0:T(1024)S(1)} %bitcast.24), kind=kLoop, calls=%fused_computation.14 | loop fusion | flops 9437056 | bytes 21103104 | tf_op jit(solution)/shard_map/reduce_sum | solution.py:27
  28.1 0.0 copy-done
  28.2 3.5 multiply_convert_fusion
  31.6 55.0 %all_to_all.34 = bf16[128,8,1024]{0,2,1:T(8,128)(2,1)S(1)} all-to-all(bf16[128,8,1024]{0,2,1:T(8,128)(2,1)S(1)} %bitcast.19), channel_id=1, replica_groups=mesh['seq'=8,'tp'=4] {'seq'}, dimensions={1} | all-to-all | bytes 4194304 | tf_op jit(solution)/shard_map/all_to_all | solution.py:29
  86.6 2.6 copy.15
  89.2 22.3 %fusion.4 = bf16[1024,7168]{1,0:T(8,128)(2,1)} fusion(bf16[1024,1024]{1,0:T(8,128)(2,1)} %bitcast.22, bf16[1024,3584]{1,0:T(8,128)(2,1)} %param.10, bf16[1024,3584]{1,0:T(8,128)(2,1)} %param.9), kind=kOutput, calls=%fused_computation.4 | convolution fusion | flops 15069085696 | bytes 31457280 | tf_op jit(solution)/shard_map/dot_general | solution.py:33
  111.6 0.0 reduce-scatter.3.cloned.1.call-update
  111.6 0.0 all-gather.2.cloned.1.call-start
  111.6 148.0 %reduce-scatter.3.cloned.1.call-done = bf16[128,7168]{1,0:T(8,128)(2,1)} async-done(((bf16[1024,7168]{1,0:T(8,128)(2,1)}), bf16[128,7168]{1,0:T(8,128)(2,1)}) %reduce-scatter.3.cloned.1.call-update) | async-done | bytes 1835024 | tf_op jit(solution)/shard_map/reduce_scatter | solution.py:32
  259.6 1.9 convert_element_type.24
  261.5 1.4 fusion.10
  262.9 0.0 all-gather.2.cloned.1.call-update
  263.0 0.0 reduce-scatter.5.cloned.1.call-start
  263.0 71.9 %all-gather.2.cloned.1.call-done = bf16[1024,3584]{1,0:T(8,128)(2,1)} async-done(((bf16[128,3584]{1,0:T(8,128)(2,1)}), bf16[1024,3584]{1,0:T(8,128)(2,1)}) %all-gather.2.cloned.1.call-update) | async-done | bytes 7340048 | tf_op jit(solution)/shard_map/all_gather | solution.py:40
  334.9 13.2 %convolution_convert_fusion = bf16[1024,1024]{1,0:T(8,128)(2,1)} fusion(bf16[1024,3584]{1,0:T(8,128)(2,1)} %all-gather.2.cloned.1.call-done, bf16[3584,1024]{1,0:T(8,128)(2,1)} %param.11), kind=kOutput, calls=%fused_computation.15 | convolution fusion | flops 7517241344 | bytes 16777216 | tf_op jit(solution)/shard_map/dot_general | solution.py:39
  348.1 0.0 reduce-scatter.5.cloned.1.call-update
  348.1 33.9 %reduce-scatter.5.cloned.1.call-done = bf16[8,32,1024]{2,1,0:T(8,128)(2,1)} async-done(((bf16[8,128,1024]{2,1,0:T(8,128)(2,1)}), bf16[8,32,1024]{2,1,0:T(8,128)(2,1)}) %reduce-scatter.5.cloned.1.call-update) | async-done | bytes 524304 | tf_op jit(solution)/shard_map/reduce_scatter | solution.py:46
  382.1 19.9 %all_to_all.35 = bf16[8,32,1024]{2,1,0:T(8,128)(2,1)S(1)} all-to-all(bf16[8,32,1024]{2,1,0:T(8,128)(2,1)} %reduce-scatter.5.cloned.1.call-done), channel_id=1, replica_groups=mesh['seq'=8,'tp'=4] {'seq'}, dimensions={0} | all-to-all | bytes 1048576 | tf_op jit(solution)/shard_map/all_to_all | solution.py:47
  402.0 0.8 copy.17
  (1 shorter events, 0.0 us)
Async XLA Ops:
  6.5 253.1 %reduce-scatter.3.cloned.1.call-start = ((), (), s32[]{:S(2)}) async-start(), calls=%async_computation.4 | async-start | bytes 16515072 | tf_op jit(solution)/shard_map/reduce_scatter | solution.py:32
  7.5 6.9 %collective-permute-start = (bf16[3,8192]{1,0:T(4,128)(2,1)S(1)}, bf16[3,8192]{1,0:T(4,128)(2,1)S(1)}, u32[]{:S(2)}, u32[]{:S(2)}) collective-permute-start(bf16[3,8192]{1,0:T(4,128)(2,1)S(1)} %slice.34), channel_id=1, source_target_pairs={{0,4},{4,8},{8,12},{12,16},{16,20},{20,24},{24,28},{1,5},{5,9},{9,... | collective-permute-start | bytes 147464 | tf_op jit(solution)/shard_map/ppermute | solution.py:10
  19.4 8.8 %copy-start = (f32[8192]{0:T(1024)S(1)}, f32[8192]{0:T(1024)}, u32[]{:S(2)}) copy-start(f32[8192]{0:T(1024)} %param.8) | copy-start | bytes 98308
  111.6 223.3 %all-gather.2.cloned.1.call-start = ((), (), s32[]{:S(2)}) async-start(), calls=%async_computation.5 | async-start | bytes 8257536 | tf_op jit(solution)/shard_map/all_gather | solution.py:40
  263.0 119.1 %reduce-scatter.5.cloned.1.call-start = ((), (), s32[]{:S(2)}) async-start(), calls=%async_computation.6 | async-start | bytes 2621440 | tf_op jit(solution)/shard_map/reduce_scatter | solution.py:46
Sparse Core Ops, SparseCore 0:
  111.7 147.8 reduce-scatter.2
  263.1 71.8 all-gather.1
  348.3 33.7 reduce-scatter.4
where the time goes:
time: 410 us; the launch traced here: 409 us
  waiting for transfers between devices  254 us (62%)
  blocking collectives  74.9 us (18%)
  matrix products  35.5 us (9%)
  other arithmetic  18.6 us (5%)
  between operations  13.2 us (3%)
  local copies, waits for them, and re-layouts  10.8 us (3%)
    reduce_scatter x1, waiting for transfers between devices, shards(): lax.psum_scatter(jnp.dot(all_rows, w_both, preferred_element_type=jnp.flo...  148 us
    all_gather x1, waiting for transfers between devices, shards(): lax.all_gather(hidden, 'seq', axis=0, tiled=True)  71.9 us
    all_to_all x1, blocking collectives, shards(): lax.all_to_all(normed, 'seq', split_axis=1, concat_axis=0, tiled=True)  55 us
    reduce_scatter x1, waiting for transfers between devices, shards(): lax.psum_scatter(out_terms.astype(jnp.bfloat16), 'tp', scatter_dimension=...  33.9 us
    dot_general x1, matrix products, shards(): jnp.dot(all_rows, w_both, preferred_element_type=jnp.float32)  22.3 us
    all_to_all x1, blocking collectives, shards(): lax.all_to_all(summed, 'seq', split_axis=0, concat_axis=2, tiled=True)  19.9 us
    dot_general x1, matrix products, shards(): jnp.dot(lax.all_gather(hidden, 'seq', axis=0, tiled=True), down_weight, p...  13.2 us
    reduce_sum x1, other arithmetic, shards(): jnp.mean(conv_out * conv_out, axis=-1, keepdims=True) + 1e-05  8.75 us
  transfers between devices with their start and end apart: 4, of which 3 were waited for; matrix products, arithmetic and copies ran while one was open for 1% of the time, Pallas kernels for 0%

commit v1 on v0

--- a/solution.py
+++ b/solution.py
@@ -2,6 +2,12 @@
 import jax.numpy as jnp
 from jax import lax
 from jax.sharding import PartitionSpec as P
+
+
+def stacked_exchange(array, axis, split, join):
+    shards = jnp.split(array, lax.axis_size(axis), axis=split)
+    received = lax.all_to_all(jnp.stack(shards), axis, 0, 0)
+    return jnp.concatenate(received, axis=join)
 
 
 def from_behind(shard, axis, by):
@@ -26,7 +32,7 @@
         conv_out = conv_out + conv_weight[tap_index][None, :] * extended[begin : begin + tok_rows]
     scale_rms = lax.rsqrt(jnp.mean(conv_out * conv_out, axis=-1, keepdims=True) + 1e-05)
     normed = (conv_out * scale_rms * norm_gain[None, :]).astype(jnp.bfloat16)
-    all_rows = lax.all_to_all(normed, "seq", split_axis=1, concat_axis=0, tiled=True)
+    all_rows = stacked_exchange(normed, "seq", 1, 0)
     half_cols = gate_weight.shape[1]
     w_both = jnp.concatenate([gate_weight, up_weight], 1)
     gate_share = lax.psum_scatter(

time: 410 us -> 394 us (0.961)
  other arithmetic: 18.6 us -> 8.2 us
  local copies, waits for them, and re-layouts: 10.8 us -> 3.22 us
    reduce_sum x1, other arithmetic: 8.75 us -> 2.21 us  [shards(): jnp.mean(conv_out * conv_out, axis=-1, keepdims=True) + 1e-05]
  transfers between devices with their start and end apart: 4 -> 4, of which waited for: 3 -> 3; matrix products, arithmetic and copies ran while one was open for 1% -> 0% of each run, Pallas kernels for 0% -> 0%
where the time goes in v1:
time: 394 us; the launch traced here: 393 us
  waiting for transfers between devices  254 us (64%)
  blocking collectives  77.3 us (20%)
  matrix products  34.9 us (9%)
  between operations  13.3 us (3%)
  other arithmetic  8.2 us (2%)
    reduce_scatter x1, waiting for transfers between devices, shards(): lax.psum_scatter(jnp.dot(all_rows, w_both, preferred_element_type=jnp.flo...  148 us
    all_gather x1, waiting for transfers between devices, shards(): lax.all_gather(hidden, 'seq', axis=0, tiled=True)  71.9 us
    all_to_all x1, blocking collectives, stacked_exchange(): received = lax.all_to_all(jnp.stack(shards), axis, 0, 0)  57.3 us
    reduce_scatter x1, waiting for transfers between devices, shards(): lax.psum_scatter(out_terms.astype(jnp.bfloat16), 'tp', scatter_dimension=...  33.9 us
    dot_general x1, matrix products, shards(): jnp.dot(all_rows, w_both, preferred_element_type=jnp.float32)  21.7 us
    all_to_all x1, blocking collectives, shards(): lax.all_to_all(summed, 'seq', split_axis=0, concat_axis=2, tiled=True)  19.9 us
    dot_general x1, matrix products, shards(): jnp.dot(lax.all_gather(hidden, 'seq', axis=0, tiled=True), down_weight, p...  13.2 us
  transfers between devices with their start and end apart: 4, of which 3 were waited for; matrix products, arithmetic and copies ran while one was open for 0% of the time, Pallas kernels for 0%

profile of v1, /device:TPU:0, one launch (start us, length us, event | category | flops | bytes accessed | tf_op | source)
XLA Modules:
  0.0 393.2 jit_solution(10092200068694339880)
XLA Ops:
  6.5 0.0 reduce-scatter.3.cloned.1.call-start
  6.5 0.9 slice.34
  7.5 2.4 collective-permute-start
  9.9 1.3 fusion.21
  11.2 0.0 collective-permute-done
  11.2 2.2 maximum_convert_fusion
  13.4 0.0 copy-start
  13.4 2.2 multiply_reduce_fusion
  15.6 0.0 copy-done
  15.6 0.0 slice-start
  15.6 0.5 multiply_convert_fusion
  16.2 0.0 slice-start.1
  16.4 57.3 %all_to_all.20 = bf16[8,128,1024]{2,1,0:T(8,128)(2,1)S(1)} all-to-all(bf16[8,128,1024]{2,1,0:T(8,128)(2,1)S(1)} %fusion.11), channel_id=1, replica_groups=mesh['seq'=8,'tp'=4] {'seq'}, dimensions={0} | all-to-all | bytes 4194304 | tf_op jit(solution)/shard_map/all_to_all | solution.py:9
  73.7 0.0 slice-done
  73.7 0.0 slice-done.1
  73.7 21.7 %fusion.4 = bf16[1024,7168]{1,0:T(8,128)(2,1)} fusion(bf16[1024,1024]{1,0:T(8,128)(2,1)S(1)} %bitcast.50, bf16[1024,3584]{1,0:T(8,128)(2,1)S(1)} %bitcast.57, bf16[1024,3584]{1,0:T(8,128)(2,1)} %param.9), kind=kOutput, calls=%fused_computation.4 | convolution fusion | flops 15069085696 | bytes 31457280 | tf_op jit(solution)/shard_map/dot_general | solution.py:39
  95.4 0.0 reduce-scatter.3.cloned.1.call-update
  95.5 0.0 all-gather.2.cloned.1.call-start
  95.5 148.0 %reduce-scatter.3.cloned.1.call-done = bf16[128,7168]{1,0:T(8,128)(2,1)} async-done(((bf16[1024,7168]{1,0:T(8,128)(2,1)}), bf16[128,7168]{1,0:T(8,128)(2,1)}) %reduce-scatter.3.cloned.1.call-update) | async-done | bytes 1835024 | tf_op jit(solution)/shard_map/reduce_scatter | solution.py:38
  243.5 1.9 convert_element_type.24
  245.3 1.4 fusion.10
  246.8 0.0 all-gather.2.cloned.1.call-update
  246.8 0.0 reduce-scatter.5.cloned.1.call-start
  246.9 71.9 %all-gather.2.cloned.1.call-done = bf16[1024,3584]{1,0:T(8,128)(2,1)} async-done(((bf16[128,3584]{1,0:T(8,128)(2,1)}), bf16[1024,3584]{1,0:T(8,128)(2,1)}) %all-gather.2.cloned.1.call-update) | async-done | bytes 7340048 | tf_op jit(solution)/shard_map/all_gather | solution.py:46
  318.8 13.2 %convolution_convert_fusion = bf16[1024,1024]{1,0:T(8,128)(2,1)} fusion(bf16[1024,3584]{1,0:T(8,128)(2,1)} %all-gather.2.cloned.1.call-done, bf16[3584,1024]{1,0:T(8,128)(2,1)} %param.11), kind=kOutput, calls=%fused_computation.15 | convolution fusion | flops 7517241344 | bytes 16777216 | tf_op jit(solution)/shard_map/dot_general | solution.py:45
  332.0 0.0 reduce-scatter.5.cloned.1.call-update
  332.0 33.9 %reduce-scatter.5.cloned.1.call-done = bf16[8,32,1024]{2,1,0:T(8,128)(2,1)} async-done(((bf16[8,128,1024]{2,1,0:T(8,128)(2,1)}), bf16[8,32,1024]{2,1,0:T(8,128)(2,1)}) %reduce-scatter.5.cloned.1.call-update) | async-done | bytes 524304 | tf_op jit(solution)/shard_map/reduce_scatter | solution.py:52
  365.9 19.9 %all_to_all.21 = bf16[8,32,1024]{2,1,0:T(8,128)(2,1)S(1)} all-to-all(bf16[8,32,1024]{2,1,0:T(8,128)(2,1)} %reduce-scatter.5.cloned.1.call-done), channel_id=1, replica_groups=mesh['seq'=8,'tp'=4] {'seq'}, dimensions={0} | all-to-all | bytes 1048576 | tf_op jit(solution)/shard_map/all_to_all | solution.py:53
  385.8 0.8 copy.8
  (10 shorter events, 0.2 us)
Async XLA Ops:
  6.5 237.0 %reduce-scatter.3.cloned.1.call-start = ((), (), s32[]{:S(2)}) async-start(), calls=%async_computation.4 | async-start | bytes 16515072 | tf_op jit(solution)/shard_map/reduce_scatter | solution.py:38
  7.5 3.7 collective-permute-start
  13.4 2.2 copy-start
  15.6 58.1 %slice-start = ((s8[7340032]{0:T(1024)(128)(4,1)}), s8[4194304]{0:T(1024)(128)(4,1)S(1)}, s32[]{:S(2)}) async-start(s8[7340032]{0:T(1024)(128)(4,1)} %bitcast.56), calls=%async_computation.7 | async-start | bytes 8388608
  16.2 57.6 %slice-start.1 = ((s8[7340032]{0:T(1024)(128)(4,1)}), s8[3145728]{0:T(1024)(128)(4,1)S(1)}, s32[]{:S(2)}) async-start(s8[7340032]{0:T(1024)(128)(4,1)} %bitcast.56), calls=%async_computation.8 | async-start | bytes 6291456
  95.5 223.3 %all-gather.2.cloned.1.call-start = ((), (), s32[]{:S(2)}) async-start(), calls=%async_computation.5 | async-start | bytes 8257536 | tf_op jit(solution)/shard_map/all_gather | solution.py:46
  246.8 119.1 %reduce-scatter.5.cloned.1.call-start = ((), (), s32[]{:S(2)}) async-start(), calls=%async_computation.6 | async-start | bytes 2621440 | tf_op jit(solution)/shard_map/reduce_scatter | solution.py:52
Sparse Core Ops, SparseCore 0:
  95.6 147.8 reduce-scatter.2
  246.9 71.8 all-gather.1
  332.1 33.7 reduce-scatter.4
